TPU v7x, 32 devices: a whole 2x2x4 slice. The times are simulated.
32 devices in a mesh: gz: 2 (over x), row: 4 (over y, core), col: 4 (over z).
Axes of the slice: x: 2, y: 2, z: 4, core: 2. Of those that a mesh axis runs over, the one named last changes fastest.
Arguments:
- sections: bfloat16 [4, 2048, 2048], P('gz', 'row', 'col'), may hold values from -6 to 6
- priors: int32 [2, 4, 8, 8], P(None, 'gz', 'row', 'col'), may hold values from -64 to 64
- row_order: int32 [8], replicated, may hold values from 0 to 7, each once
Outputs:
- mesh_flows: float32 [8, 64], P('row')
Inputs may be any that keep to these rules, and one draw needn't show every extreme that they name: A permutation of the patch rows: mesh row m holds patch row row_order[m].
All inputs are finite; a program needn't handle non-finite values.
Results may differ from a plain program's by a relative error of at most 0.0003.
Values may be sent and summed in bfloat16 or wider, within the bound.
A program may use at most 64 MiB of HBM per device.

v0:
```python
import math

import jax
import jax.numpy as jnp
import numpy as np
from jax import lax
from jax.experimental import pallas as pl
from jax.experimental.pallas import tpu as pltpu
from jax.sharding import PartitionSpec as P

PATCH = 512
STRIDE = 256
LAGS = 128
HALO = 256
HALF = PATCH // 2
QUARTER = PATCH // 4
KROWS = HALF + 16


def angle_of(products):
    return (products % PATCH) * (2.0 * math.pi / PATCH)


def dft_table():
    k = np.arange(HALF)[:, None]
    x = np.arange(PATCH)[None, :]
    table = np.zeros((2 * KROWS, PATCH))
    table[:HALF] = np.cos(angle_of(k * x))
    table[HALF] = np.cos(angle_of(HALF * x[0]))
    table[KROWS : KROWS + HALF] = -np.sin(angle_of(k * x))
    return table


def split_tables():
    y = np.arange(QUARTER)[:, None]
    blocks = []
    for g in range(4):
        l = 4 * np.arange(QUARTER)[None, :] + g
        c, s = np.cos(angle_of(y * l)), np.sin(angle_of(y * l))
        blocks.append(np.block([[c, -s], [s, c]]))
    return np.stack(blocks)


def lag_tables():
    lag = np.arange(2 * LAGS)[:, None] - LAGS
    l = np.concatenate([4 * np.arange(QUARTER) + g for g in range(4)])[None, :]
    k = np.arange(KROWS)[None, :]
    weight = np.where(k == 0, 1.0, np.where(k < HALF, 2.0, np.where(k == HALF, 1.0, 0.0)))
    col = (np.cos(angle_of(lag * l)), np.sin(angle_of(lag * l)))
    row_cos = np.cos(angle_of(lag * k)) * weight
    row_sin = -np.sin(angle_of(lag * k)) * weight
    row = np.concatenate([row_cos, row_sin], axis=1)
    return col[0], col[1], row


def bf16_const(value):
    return value.astype(np.float32).astype(jnp.bfloat16)


def f32_const(value):
    return bf16_const(value).astype(np.float32)


def first_pass(ext, section, i, dft_ref, pq_ref, slot, outer):
    rows = pl.ds(pl.multiple_of(i * STRIDE, STRIDE), PATCH)
    edge, far = HALO // 2, ext.shape[2] - HALO // 2
    if not outer:
        pq_ref[slot, :, edge:far] = jnp.dot(
            dft_ref[...], ext[section, rows, edge:far], preferred_element_type=jnp.float32
        )
        return
    window = jnp.concatenate([ext[section, rows, :edge], ext[section, rows, far:]], axis=1)
    both = jnp.dot(dft_ref[...], window, preferred_element_type=jnp.float32)
    pq_ref[slot, :, :edge] = both[:, :edge]
    pq_ref[slot, :, far:] = both[:, edge:]


def spectrum_pair(wg_ref, spec_ref, pq_ref, slot, base):
    for j in range(2):
        p, q = [], []
        for t in range(4):
            lanes = slice(j * STRIDE + t * QUARTER, j * STRIDE + (t + 1) * QUARTER)
            p.append(pq_ref[slot, :KROWS, lanes])
            q.append(pq_ref[slot, KROWS:, lanes])
        ps, pd, qs, qd = p[0] + p[2], p[0] - p[2], q[0] + q[2], q[0] - q[2]
        pt, pu, qt, qu = p[1] + p[3], p[1] - p[3], q[1] + q[3], q[1] - q[3]
        groups = ((ps + pt, qs + qt), (pd + qu, qd - pu), (ps - pt, qs - qt), (pd - qu, qd + pu))
        for g, (real, imag) in enumerate(groups):
            left = jnp.concatenate([real.astype(jnp.bfloat16), imag.astype(jnp.bfloat16)], axis=1)
            out = jnp.dot(left, wg_ref[g], preferred_element_type=jnp.float32).astype(jnp.bfloat16)
            lo = g * QUARTER
            spec_ref[base + j, :, lo : lo + QUARTER] = out[:, :QUARTER]
            spec_ref[base + j, :, PATCH + lo : PATCH + lo + QUARTER] = out[:, QUARTER:]


def lag_rows(table, prior):
    tiles = [
        table[t, pl.ds(prior + LAGS // 2, LAGS), :].astype(jnp.bfloat16)
        for t in range(table.shape[0])
    ]
    return jnp.concatenate(tiles, axis=1)


def lane_tiles(table):
    width = -(-table.shape[1] // LAGS) * LAGS
    table = np.pad(table, ((0, 0), (0, width - table.shape[1])))
    return np.stack(np.split(table, width // LAGS, axis=1))


def pair_flow(first, second, p, q, spec_ref, colc_ref, cols_ref, row_ref):
    f32 = jnp.float32
    ar = spec_ref[first, :, :PATCH].astype(f32)
    ai = spec_ref[first, :, PATCH:].astype(f32)
    br = spec_ref[second, :, :PATCH].astype(f32)
    bi = spec_ref[second, :, PATCH:].astype(f32)
    cr = (ar * br + ai * bi).astype(jnp.bfloat16)
    ci = (ar * bi - ai * br).astype(jnp.bfloat16)
    ec = lag_rows(colc_ref, q)
    es = lag_rows(cols_ref, q)
    left = jnp.concatenate([cr, ci], axis=1)
    right = jnp.concatenate(
        [jnp.concatenate([ec, -es], axis=1), jnp.concatenate([es, ec], axis=1)], axis=0
    )
    half = lax.dot_general(
        left, right, (((1,), (1,)), ((), ())), preferred_element_type=f32
    ).astype(jnp.bfloat16)
    stacked = jnp.concatenate([half[:, :LAGS], half[:, LAGS:]], axis=0)
    rows = lag_rows(row_ref, p)[:, : 2 * KROWS]
    surface = jnp.dot(rows, stacked, preferred_element_type=f32) * (1.0 / PATCH**3)
    w = surface * surface
    da = (lax.broadcasted_iota(jnp.int32, (LAGS, LAGS), 0) - LAGS // 2).astype(f32)
    db = (lax.broadcasted_iota(jnp.int32, (1, LAGS), 1) - LAGS // 2).astype(f32)
    col_w = jnp.sum(w, axis=0, keepdims=True)
    total = 1.0 + jnp.sum(col_w, axis=1, keepdims=True)
    row_m = jnp.sum(jnp.sum(w * da, axis=0, keepdims=True), axis=1, keepdims=True)
    col_m = jnp.sum(col_w * db, axis=1, keepdims=True)
    return p.astype(f32) + row_m / total, q.astype(f32) + col_m / total


def make_kernel(sizes, rows_each):
    size_gz, size_row, size_col = sizes
    count = size_gz * size_row * size_col
    side = 2 * STRIDE
    margin = HALO // 2
    far = side - margin
    mesh_id = pl.DeviceIdType.MESH
    steps = [(a, b) for a in (-1, 0, 1) for b in (-1, 0, 1) if (a, b) != (0, 0)]
    halo_span = {-1: (0, margin), 0: (margin, side), 1: (margin + side, margin)}
    edge_span = {-1: (0, margin), 0: (0, side), 1: (far, margin)}
    chunks = (
        (0, side, 0, margin),
        (0, side, far, margin),
        (0, margin, margin, far - margin),
        (far, margin, margin, far - margin),
        (margin, far - margin, margin, far - margin),
    )
    needs = {(0, -1): 1, (-1, -1): 1, (1, -1): 1, (0, 1): 2, (-1, 1): 2, (1, 1): 2, (-1, 0): 3}
    needs[(1, 0)] = 4

    def kernel(
        pri_ref, order_ref, sec_hbm, dft_hbm, wg_hbm, colc_hbm, cols_hbm, row_hbm, out_ref,
        ext, dft_ref, wg_ref, colc_ref, cols_ref, row_ref, spec_ref, pq_ref, mine_ref, all_ref,
        load_sem, own_send, own_recv, next_send, next_recv, chunk_send, chunk_recv, flow_send,
        flow_recv,
    ):
        gz, row, col = lax.axis_index("gz"), lax.axis_index("row"), lax.axis_index("col")
        flat = (gz * size_row + row) * size_col + col

        def device(number):
            return (
                number // (size_row * size_col),
                (number // size_col) % size_row,
                number % size_col,
            )

        loads = [
            pltpu.make_async_copy(
                sec_hbm, ext.at[0:2, margin : margin + side, margin : margin + side],
                load_sem.at[0],
            )
        ]
        tables = (
            (dft_hbm, dft_ref), (wg_hbm, wg_ref), (colc_hbm, colc_ref), (cols_hbm, cols_ref),
            (row_hbm, row_ref),
        )
        for n, (source, target) in enumerate(tables):
            loads.append(pltpu.make_async_copy(source, target, load_sem.at[n + 1]))
        for copy in loads:
            copy.start()

        barrier = pltpu.get_barrier_semaphore()

        def greet(n, carry):
            other = (flat + n) % count
            pl.semaphore_signal(barrier, 1, device_id=device(other), device_id_type=mesh_id)
            return carry

        lax.fori_loop(1, count, greet, 0)

        def exists(step):
            a, b = step
            ok = None
            for delta, place, size in ((a, row, size_row), (b, col, size_col)):
                if delta:
                    this = place > 0 if delta < 0 else place < size - 1
                    ok = this if ok is None else jnp.logical_and(ok, this)
            return ok

        def region(step):
            (r0, rn), (c0, cn) = halo_span[step[0]], halo_span[step[1]]
            return slice(r0, r0 + rn), slice(c0, c0 + cn)

        def edge(step, offset):
            (r0, rn), (c0, cn) = edge_span[step[0]], edge_span[step[1]]
            return slice(r0 + offset, r0 + rn + offset), slice(c0 + offset, c0 + cn + offset)

        def own_copy(n):
            step = steps[n]
            back = (-step[0], -step[1])
            return pltpu.make_async_remote_copy(
                src_ref=sec_hbm.at[(slice(0, 2), *edge(step, 0))],
                dst_ref=ext.at[(slice(0, 2), *region(back))],
                send_sem=own_send.at[n], recv_sem=own_recv.at[steps.index(back)],
                device_id=(gz, row + step[0], col + step[1]), device_id_type=mesh_id,
            )

        def next_copy(n):
            step = steps[n]
            back = (-step[0], -step[1])
            return pltpu.make_async_remote_copy(
                src_ref=ext.at[(2, *edge(step, margin))],
                dst_ref=ext.at[(2, *region(back))],
                send_sem=next_send.at[n], recv_sem=next_recv.at[steps.index(back)],
                device_id=(gz, row + step[0], col + step[1]), device_id_type=mesh_id,
            )

        def own_wait(n):
            ref = ext.at[(slice(0, 2), *region(steps[n]))]
            pltpu.make_async_copy(ref, ref, own_recv.at[n]).wait()

        def next_wait(n):
            ref = ext.at[(2, *region(steps[n]))]
            pltpu.make_async_copy(ref, ref, next_recv.at[n]).wait()

        def chunk_copy(n):
            r0, rn, c0, cn = chunks[n]
            return pltpu.make_async_remote_copy(
                src_ref=sec_hbm.at[0, r0 : r0 + rn, c0 : c0 + cn],
                dst_ref=ext.at[
                    2, margin + r0 : margin + r0 + rn, margin + c0 : margin + c0 + cn
                ],
                send_sem=chunk_send.at[n], recv_sem=chunk_recv.at[n],
                device_id=((gz + size_gz - 1) % size_gz, row, col), device_id_type=mesh_id,
            )

        def forward(low, high):
            for n in range(low, high):
                chunk_copy(n).wait_recv()
                for m, step in enumerate(steps):
                    if needs[step] == n + 1:
                        @pl.when(exists(step))
                        def _(m=m):
                            next_copy(m).start()

        def halo_waits(wait, outer):
            for n, step in enumerate(steps):
                if (step[1] != 0) == outer:
                    @pl.when(exists(step))
                    def _(n=n):
                        wait(n)

        def middle(n, carry):
            first_pass(ext, n // 2, n % 2, dft_ref, pq_ref, n % 4, False)
            return carry

        def spectra(n, carry):
            first_pass(ext, n // 2, n % 2, dft_ref, pq_ref, n % 4, True)
            spectrum_pair(wg_ref, spec_ref, pq_ref, n % 4, n * 2)
            return carry

        for n, step in enumerate(steps):
            @pl.when(jnp.logical_not(exists(step)))
            def _(step=step):
                rows, cols = region(step)
                ext[:, rows, cols] = jnp.zeros(
                    (3, rows.stop - rows.start, cols.stop - cols.start), ext.dtype
                )

        mine_ref[...] = jnp.zeros_like(mine_ref)
        pl.semaphore_wait(barrier, count - 1)
        for n in range(len(chunks)):
            chunk_copy(n).start()
        for n, step in enumerate(steps):
            @pl.when(exists(step))
            def _(n=n):
                own_copy(n).start()
        for copy in loads:
            copy.wait()
        halo_waits(own_wait, False)
        lax.fori_loop(0, 4, middle, 0, unroll=2)
        forward(0, 2)
        halo_waits(own_wait, True)

        lane = lax.broadcasted_iota(jnp.int32, (1, LAGS), 1)
        sections, columns = 2 * size_gz, 2 * size_col

        def prior(part, n):
            return pri_ref[part, n // 4, (n // 2) % 2, n % 2]

        def pairs_static(low, high):
            values = []
            for n in range(low, high):
                a, b = pair_flow(
                    n, n + 4, prior(0, n), prior(1, n), spec_ref, colc_ref, cols_ref, row_ref
                )
                at = (2 * gz + n // 4) * columns + 2 * col + n % 2
                values.append(
                    jnp.where(lane == at, a, 0.0)
                    + jnp.where(lane == at + sections * columns, b, 0.0)
                )
            mine_ref[0] = mine_ref[0] + values[0] + values[1]
            mine_ref[1] = mine_ref[1] + values[2] + values[3]

        lax.fori_loop(0, 4, spectra, 0, unroll=2)
        forward(2, 4)
        pairs_static(0, 4)
        forward(4, 5)
        halo_waits(next_wait, False)
        lax.fori_loop(4, 6, middle, 0, unroll=2)
        halo_waits(next_wait, True)
        lax.fori_loop(4, 6, spectra, 0, unroll=2)
        pairs_static(4, 8)

        total_rows = 2 * size_row
        slot = gz * size_col + col
        place = slot * total_rows + 2 * row

        def flow_copy(n):
            return pltpu.make_async_remote_copy(
                src_ref=mine_ref, dst_ref=all_ref.at[pl.ds(place, 2)],
                send_sem=flow_send, recv_sem=flow_recv,
                device_id=device((flat + n) % count), device_id_type=mesh_id,
            )

        def send(n, carry):
            flow_copy(n).start()
            return carry

        lax.fori_loop(1, count, send, 0)
        all_ref[place] = mine_ref[0]
        all_ref[place + 1] = mine_ref[1]
        for n in range(len(chunks)):
            chunk_copy(n).wait_send()
        for n, step in enumerate(steps):
            @pl.when(exists(step))
            def _(n=n):
                own_copy(n).wait_send()
                next_copy(n).wait_send()
        got = all_ref.at[pl.ds(0, 2 * (count - 1))]
        pltpu.make_async_copy(got, got, flow_recv).wait()
        for m in range(rows_each):
            wanted = order_ref[row * rows_each + m]
            value = all_ref[wanted]
            for other in range(1, size_gz * size_col):
                value = value + all_ref[other * total_rows + wanted]
            out_ref[m : m + 1, :] = value[:, : out_ref.shape[1]]
        pltpu.make_async_copy(got, got, flow_send).wait()

    return kernel


def body(sections, priors, row_order):
    sizes = tuple(lax.axis_size(name) for name in ("gz", "row", "col"))
    count = math.prod(sizes)
    rows_each = row_order.shape[0] // sizes[1]
    width = 2 * 2 * sizes[0] * 2 * sizes[2]
    colc, cols, row = lag_tables()
    tables = (
        bf16_const(dft_table()),
        bf16_const(split_tables()),
        f32_const(lane_tiles(colc)),
        f32_const(lane_tiles(cols)),
        f32_const(lane_tiles(row)),
    )
    smem = pl.BlockSpec(memory_space=pltpu.SMEM)
    hbm = pl.BlockSpec(memory_space=pl.ANY)
    dma = pltpu.SemaphoreType.DMA
    wide = 2 * STRIDE + HALO
    flows = pl.pallas_call(
        make_kernel(sizes, rows_each),
        out_shape=jax.ShapeDtypeStruct((rows_each, width), jnp.float32),
        in_specs=[smem, smem] + [hbm] * 6,
        out_specs=pl.BlockSpec(memory_space=pltpu.VMEM),
        scratch_shapes=[
            pltpu.VMEM((3, wide, wide), jnp.bfloat16),
            *[pltpu.VMEM(t.shape, t.dtype) for t in tables],
            pltpu.VMEM((12, KROWS, 2 * PATCH), jnp.bfloat16),
            pltpu.VMEM((4, 2 * KROWS, wide), jnp.float32),
            pltpu.VMEM((2, 1, LAGS), jnp.float32),
            pltpu.VMEM((2 * count, 1, LAGS), jnp.float32),
            dma((6,)), dma((8,)), dma((8,)), dma((8,)), dma((8,)), dma((5,)), dma((5,)),
            dma(()), dma(()),
        ],
        compiler_params=pltpu.CompilerParams(
            vmem_limit_bytes=67043328, collective_id=0, has_side_effects=True
        ),
    )(priors, row_order, sections, *tables)
    return flows


def solution(mesh):
    placed = (P("gz", "row", "col"), P(None, "gz", "row", "col"), P())
    return jax.shard_map(
        body, mesh=mesh, in_specs=placed, out_specs=P("row", None), check_vma=False
    )
```

profile of v0, /device:TPU:0, one launch (start us, length us, event | category | flops | bytes accessed | tf_op | source)
XLA Modules:
  0.0 34.9 jit_solution(305105481092341007)
XLA Ops:
  0.0 33.7 %shard_map.82 = f32[2,64]{1,0:T(2,128)} custom-call(s32[2,2,2,2]{3,2,1,0:T(2,128)} %pri_ref.1, s32[8]{0:T(128)} %order_ref.1, bf16[2,512,512]{2,1,0:T(8,128)(2,1)} %sec_hbm.1, bf16[544,512]{1,0:T(8,128)(2,1)} %constant.10.clone.dft_hbm, bf16[4,256,256]{2,1,0:T(8,128)(2,1)} %constant.11.clone.wg_hbm, f32[4,256,128]{2,1,0:T(8,128)} %constant.12.clone.colc_hbm, ...), custom_call_target="tpu_custom_call" | custom-call | tf_op jit(solution)/shard_map/pallas_call | solution.py:389
  33.7 1.2 %copy.10 = f32[2,64]{1,0:T(2,128)} copy(f32[2,64]{1,0:T(2,128)} %shard_map.82) | data formatting | bytes 1024
where the time goes:
time: 35.1 us; the launch traced here: 34.9 us
  Pallas kernels  33.7 us (96%)
  local copies, waits for them, and re-layouts  1.24 us (4%)
    pallas_call x1, Pallas kernels, body(): pl.pallas_call(make_kernel(sizes, rows_each), out_shape=jax.ShapeDtypeStr...  33.7 us
    unnamed x1, local copies, waits for them, and re-layouts  1.24 us

commit v1 on v0

--- a/solution.py
+++ b/solution.py
@@ -143,25 +143,32 @@
     side = 2 * STRIDE
     margin = HALO // 2
     far = side - margin
+    inner = far - margin
     mesh_id = pl.DeviceIdType.MESH
-    steps = [(a, b) for a in (-1, 0, 1) for b in (-1, 0, 1) if (a, b) != (0, 0)]
-    halo_span = {-1: (0, margin), 0: (margin, side), 1: (margin + side, margin)}
-    edge_span = {-1: (0, margin), 0: (0, side), 1: (far, margin)}
+    cross = ((-1, 0), (1, 0), (0, -1), (0, 1))
+    diagonal = ((-1, -1), (-1, 1), (1, -1), (1, 1))
+    partners = sorted({1 % size_gz, size_gz - 1} - {0})
+    reaches = doubling(sizes)
+    rounds = len(reaches) + 2
+    span = {-1: (0, margin), 0: (0, side), 1: (far, margin)}
+    halo = {-1: (-margin, margin), 0: (0, side), 1: (side, margin)}
     chunks = (
-        (0, side, 0, margin),
-        (0, side, far, margin),
-        (0, margin, margin, far - margin),
-        (far, margin, margin, far - margin),
-        (margin, far - margin, margin, far - margin),
+        (0, margin, 0, margin), (0, margin, far, margin),
+        (far, margin, 0, margin), (far, margin, far, margin),
+        (margin, inner, 0, margin), (margin, inner, far, margin),
+        (0, margin, margin, inner), (far, margin, margin, inner),
+        (margin, inner, margin, inner),
     )
-    needs = {(0, -1): 1, (-1, -1): 1, (1, -1): 1, (0, 1): 2, (-1, 1): 2, (1, 1): 2, (-1, 0): 3}
-    needs[(1, 0)] = 4
+    copies = halo_copies(span, halo, margin, inner, cross, diagonal)
+
+    def pick(section, *kinds):
+        return [n for n, c in enumerate(copies) if c[0] == section and c[1] in kinds]
 
     def kernel(
-        pri_ref, order_ref, sec_hbm, dft_hbm, wg_hbm, colc_hbm, cols_hbm, row_hbm, out_ref,
+        pri_hbm, order_hbm, sec_hbm, dft_hbm, wg_hbm, colc_hbm, cols_hbm, row_hbm, out_ref,
         ext, dft_ref, wg_ref, colc_ref, cols_ref, row_ref, spec_ref, pq_ref, mine_ref, all_ref,
-        load_sem, own_send, own_recv, next_send, next_recv, chunk_send, chunk_recv, flow_send,
-        flow_recv,
+        load_sem, halo_send, halo_recv, chunk_send, chunk_recv, flow_send, flow_recv, flood, pri_ref,
+        order_ref,
     ):
         gz, row, col = lax.axis_index("gz"), lax.axis_index("row"), lax.axis_index("col")
         flat = (gz * size_row + row) * size_col + col
@@ -172,30 +179,6 @@
                 (number // size_col) % size_row,
                 number % size_col,
             )
-
-        loads = [
-            pltpu.make_async_copy(
-                sec_hbm, ext.at[0:2, margin : margin + side, margin : margin + side],
-                load_sem.at[0],
-            )
-        ]
-        tables = (
-            (dft_hbm, dft_ref), (wg_hbm, wg_ref), (colc_hbm, colc_ref), (cols_hbm, cols_ref),
-            (row_hbm, row_ref),
-        )
-        for n, (source, target) in enumerate(tables):
-            loads.append(pltpu.make_async_copy(source, target, load_sem.at[n + 1]))
-        for copy in loads:
-            copy.start()
-
-        barrier = pltpu.get_barrier_semaphore()
-
-        def greet(n, carry):
-            other = (flat + n) % count
-            pl.semaphore_signal(barrier, 1, device_id=device(other), device_id_type=mesh_id)
-            return carry
-
-        lax.fori_loop(1, count, greet, 0)
 
         def exists(step):
             a, b = step
@@ -206,68 +189,126 @@
                     ok = this if ok is None else jnp.logical_and(ok, this)
             return ok
 
-        def region(step):
-            (r0, rn), (c0, cn) = halo_span[step[0]], halo_span[step[1]]
-            return slice(r0, r0 + rn), slice(c0, c0 + cn)
-
-        def edge(step, offset):
-            (r0, rn), (c0, cn) = edge_span[step[0]], edge_span[step[1]]
-            return slice(r0 + offset, r0 + rn + offset), slice(c0 + offset, c0 + cn + offset)
-
-        def own_copy(n):
-            step = steps[n]
-            back = (-step[0], -step[1])
+        near = len(partners)
+        for step in cross:
+            near = near + exists(step).astype(jnp.int32)
+
+        def greet():
+            barrier = pltpu.get_barrier_semaphore()
+            for other in partners:
+                pl.semaphore_signal(
+                    barrier, 1, device_id=((gz + other) % size_gz, row, col),
+                    device_id_type=mesh_id,
+                )
+            for step in cross:
+                @pl.when(exists(step))
+                def _(step=step):
+                    pl.semaphore_signal(
+                        barrier, 1, device_id=(gz, row + step[0], col + step[1]),
+                        device_id_type=mesh_id,
+                    )
+
+
+        greet()
+        loads = [
+            pltpu.make_async_copy(
+                sec_hbm.at[n], ext.at[n, margin : margin + side, margin : margin + side],
+                load_sem.at[n],
+            )
+            for n in range(2)
+        ]
+        tables = (
+            (dft_hbm, dft_ref), (wg_hbm, wg_ref), (colc_hbm, colc_ref), (cols_hbm, cols_ref),
+            (row_hbm, row_ref), (pri_hbm, pri_ref), (order_hbm, order_ref),
+        )
+        for n, (source, target) in enumerate(tables):
+            loads.append(pltpu.make_async_copy(source, target, load_sem.at[n + 2]))
+        for copy in loads:
+            copy.start()
+
+        def place(section, r0, rn, c0, cn):
+            return ext.at[
+                section, margin + r0 : margin + r0 + rn, margin + c0 : margin + c0 + cn
+            ]
+
+        def landing(n):
+            section, _, (a, b), _, (r0, rn, c0, cn) = copies[n]
+            return place(section, r0 - a * side, rn, c0 - b * side, cn)
+
+        def halo_copy(n):
+            section, _, (a, b), _, box = copies[n]
             return pltpu.make_async_remote_copy(
-                src_ref=sec_hbm.at[(slice(0, 2), *edge(step, 0))],
-                dst_ref=ext.at[(slice(0, 2), *region(back))],
-                send_sem=own_send.at[n], recv_sem=own_recv.at[steps.index(back)],
-                device_id=(gz, row + step[0], col + step[1]), device_id_type=mesh_id,
+                src_ref=place(section, *box), dst_ref=landing(n),
+                send_sem=halo_send.at[n], recv_sem=halo_recv.at[n],
+                device_id=(gz, row + a, col + b), device_id_type=mesh_id,
             )
 
-        def next_copy(n):
-            step = steps[n]
-            back = (-step[0], -step[1])
+        def guard(n, sign):
+            (a, b), side_col = copies[n][2], copies[n][3]
+            return exists((sign * a, side_col if side_col else sign * b))
+
+        def send(numbers):
+            for n in numbers:
+                @pl.when(guard(n, 1))
+                def _(n=n):
+                    halo_copy(n).start()
+
+        def arrive(numbers):
+            for n in numbers:
+                @pl.when(guard(n, -1))
+                def _(n=n):
+                    ref = landing(n)
+                    pltpu.make_async_copy(ref, ref, halo_recv.at[n]).wait()
+
+        def chunk_copy(n):
             return pltpu.make_async_remote_copy(
-                src_ref=ext.at[(2, *edge(step, margin))],
-                dst_ref=ext.at[(2, *region(back))],
-                send_sem=next_send.at[n], recv_sem=next_recv.at[steps.index(back)],
-                device_id=(gz, row + step[0], col + step[1]), device_id_type=mesh_id,
-            )
-
-        def own_wait(n):
-            ref = ext.at[(slice(0, 2), *region(steps[n]))]
-            pltpu.make_async_copy(ref, ref, own_recv.at[n]).wait()
-
-        def next_wait(n):
-            ref = ext.at[(2, *region(steps[n]))]
-            pltpu.make_async_copy(ref, ref, next_recv.at[n]).wait()
-
-        def chunk_copy(n):
-            r0, rn, c0, cn = chunks[n]
-            return pltpu.make_async_remote_copy(
-                src_ref=sec_hbm.at[0, r0 : r0 + rn, c0 : c0 + cn],
-                dst_ref=ext.at[
-                    2, margin + r0 : margin + r0 + rn, margin + c0 : margin + c0 + cn
-                ],
+                src_ref=place(0, *chunks[n]), dst_ref=place(2, *chunks[n]),
                 send_sem=chunk_send.at[n], recv_sem=chunk_recv.at[n],
                 device_id=((gz + size_gz - 1) % size_gz, row, col), device_id_type=mesh_id,
             )
 
-        def forward(low, high):
+        def took(low, high):
             for n in range(low, high):
                 chunk_copy(n).wait_recv()
-                for m, step in enumerate(steps):
-                    if needs[step] == n + 1:
-                        @pl.when(exists(step))
-                        def _(m=m):
-                            next_copy(m).start()
-
-        def halo_waits(wait, outer):
-            for n, step in enumerate(steps):
-                if (step[1] != 0) == outer:
-                    @pl.when(exists(step))
-                    def _(n=n):
-                        wait(n)
+
+        def rung(n):
+            if n < len(reaches):
+                k = reaches[n]
+                lines = []
+                for way in (-k, k):
+                    for axis, at, size in ((1, row, size_row), (2, col, size_col)):
+                        ok = at + way >= 0 if way < 0 else at + way < size
+                        lines.append((ok, (gz, row + way, col) if axis == 1 else (gz, row, col + way)))
+                return lines
+            if n == len(reaches):
+                return [(None, (gz, row, (col + j) % size_col)) for j in range(1, size_col)]
+            return [(None, ((gz + j) % size_gz, row, col)) for j in range(1, size_gz)]
+
+        def climb(n):
+            for ok, target in rung(n):
+                def tell(target=target):
+                    pl.semaphore_signal(
+                        flood.at[n], 1, device_id=target, device_id_type=mesh_id
+                    )
+                if ok is None:
+                    tell()
+                else:
+                    pl.when(ok)(tell)
+
+        def heard(n):
+            total = 0
+            for ok, _ in rung(n):
+                total = total + (1 if ok is None else ok.astype(jnp.int32))
+            return total
+
+        done = [0]
+
+        def spread(upto):
+            for n in range(done[0], min(upto, rounds)):
+                pl.semaphore_wait(flood.at[n], heard(n))
+                if n + 1 < rounds:
+                    climb(n + 1)
+            done[0] = max(done[0], min(upto, rounds))
 
         def middle(n, carry):
             first_pass(ext, n // 2, n % 2, dft_ref, pq_ref, n % 4, False)
@@ -278,28 +319,25 @@
             spectrum_pair(wg_ref, spec_ref, pq_ref, n % 4, n * 2)
             return carry
 
-        for n, step in enumerate(steps):
+        for step in cross + diagonal:
             @pl.when(jnp.logical_not(exists(step)))
             def _(step=step):
-                rows, cols = region(step)
-                ext[:, rows, cols] = jnp.zeros(
-                    (3, rows.stop - rows.start, cols.stop - cols.start), ext.dtype
+                (r0, rn), (c0, cn) = halo[step[0]], halo[step[1]]
+                ext[:, margin + r0 : margin + r0 + rn, margin + c0 : margin + c0 + cn] = (
+                    jnp.zeros((3, rn, cn), ext.dtype)
                 )
 
         mine_ref[...] = jnp.zeros_like(mine_ref)
-        pl.semaphore_wait(barrier, count - 1)
+        pl.semaphore_wait(pltpu.get_barrier_semaphore(), near)
+        loads[0].wait()
         for n in range(len(chunks)):
             chunk_copy(n).start()
-        for n, step in enumerate(steps):
-            @pl.when(exists(step))
-            def _(n=n):
-                own_copy(n).start()
-        for copy in loads:
+        send(pick(0, "row", "col"))
+        loads[1].wait()
+        send(pick(1, "row", "col"))
+        climb(0)
+        for copy in loads[2:]:
             copy.wait()
-        halo_waits(own_wait, False)
-        lax.fori_loop(0, 4, middle, 0, unroll=2)
-        forward(0, 2)
-        halo_waits(own_wait, True)
 
         lane = lax.broadcasted_iota(jnp.int32, (1, LAGS), 1)
         sections, columns = 2 * size_gz, 2 * size_col
@@ -321,41 +359,64 @@
             mine_ref[0] = mine_ref[0] + values[0] + values[1]
             mine_ref[1] = mine_ref[1] + values[2] + values[3]
 
-        lax.fori_loop(0, 4, spectra, 0, unroll=2)
-        forward(2, 4)
+        arrive(pick(0, "row"))
+        lax.fori_loop(0, 2, middle, 0, unroll=2)
+        spread(1)
+        took(0, 4)
+        send(pick(2, "diagonal", "corner"))
+        arrive(pick(0, "col"))
+        send(pick(0, "turn"))
+        arrive(pick(1, "row"))
+        lax.fori_loop(2, 4, middle, 0, unroll=2)
+        spread(2)
+        took(4, 5)
+        send(pick(2, "left"))
+        arrive(pick(1, "col"))
+        send(pick(1, "turn"))
+        took(5, 6)
+        send(pick(2, "right"))
+        arrive(pick(0, "turn"))
+        lax.fori_loop(0, 2, spectra, 0, unroll=2)
+        spread(3)
+        took(6, 7)
+        send(pick(2, "up"))
+        took(7, 8)
+        send(pick(2, "down"))
+        arrive(pick(1, "turn"))
+        lax.fori_loop(2, 4, spectra, 0, unroll=2)
         pairs_static(0, 4)
-        forward(4, 5)
-        halo_waits(next_wait, False)
+        took(8, 9)
+        arrive(pick(2, "up", "down", "corner"))
         lax.fori_loop(4, 6, middle, 0, unroll=2)
-        halo_waits(next_wait, True)
+        arrive(pick(2, "left", "right", "diagonal"))
         lax.fori_loop(4, 6, spectra, 0, unroll=2)
         pairs_static(4, 8)
+        spread(rounds)
 
         total_rows = 2 * size_row
         slot = gz * size_col + col
-        place = slot * total_rows + 2 * row
-
-        def flow_copy(n):
-            return pltpu.make_async_remote_copy(
-                src_ref=mine_ref, dst_ref=all_ref.at[pl.ds(place, 2)],
-                send_sem=flow_send, recv_sem=flow_recv,
-                device_id=device((flat + n) % count), device_id_type=mesh_id,
-            )
-
-        def send(n, carry):
-            flow_copy(n).start()
-            return carry
-
-        lax.fori_loop(1, count, send, 0)
-        all_ref[place] = mine_ref[0]
-        all_ref[place + 1] = mine_ref[1]
+        spot = slot * total_rows + 2 * row
+
+        rows_on = [(row + n) % size_row for n in range(size_row)]
+        cols_on = [(col + n) % size_col for n in range(size_col)]
+        for a in range(size_gz):
+            plane = (gz + a) % size_gz
+            for b in range(size_row):
+                for c in range(size_col):
+                    if a + b + c:
+                        pltpu.make_async_remote_copy(
+                            src_ref=mine_ref, dst_ref=all_ref.at[pl.ds(spot, 2)],
+                            send_sem=flow_send, recv_sem=flow_recv,
+                            device_id=(plane, rows_on[b], cols_on[c]), device_id_type=mesh_id,
+                        ).start()
+        all_ref[spot] = mine_ref[0]
+        all_ref[spot + 1] = mine_ref[1]
         for n in range(len(chunks)):
             chunk_copy(n).wait_send()
-        for n, step in enumerate(steps):
-            @pl.when(exists(step))
+        for n in range(len(copies)):
+            @pl.when(guard(n, 1))
             def _(n=n):
-                own_copy(n).wait_send()
-                next_copy(n).wait_send()
+                halo_copy(n).wait_send()
         got = all_ref.at[pl.ds(0, 2 * (count - 1))]
         pltpu.make_async_copy(got, got, flow_recv).wait()
         for m in range(rows_each):
@@ -367,6 +428,32 @@
         pltpu.make_async_copy(got, got, flow_send).wait()
 
     return kernel
+
+
+def doubling(sizes):
+    reaches = [1]
+    while 2 * reaches[-1] < max(sizes[1:]):
+        reaches.append(2 * reaches[-1])
+    return reaches
+
+
+def halo_copies(span, halo, margin, inner, cross, diagonal):
+    copies = []
+    for section in range(2):
+        for step in cross:
+            kind = "row" if step[0] else "col"
+            copies.append((section, kind, step, 0, span[step[0]] + span[step[1]]))
+        for a, b in diagonal:
+            copies.append((section, "turn", (a, 0), b, span[a] + halo[b]))
+    for a, b in diagonal:
+        copies.append((2, "diagonal", (a, b), 0, span[a] + span[b]))
+    for a, b in diagonal:
+        copies.append((2, "corner", (a, 0), 0, span[a] + span[b]))
+    for b in (-1, 1):
+        copies.append((2, "left" if b < 0 else "right", (0, b), 0, span[0] + span[b]))
+    for a in (-1, 1):
+        copies.append((2, "up" if a < 0 else "down", (a, 0), 0, span[a] + (margin, inner)))
+    return copies
 
 
 def body(sections, priors, row_order):
@@ -382,14 +469,13 @@
         f32_const(lane_tiles(cols)),
         f32_const(lane_tiles(row)),
     )
-    smem = pl.BlockSpec(memory_space=pltpu.SMEM)
     hbm = pl.BlockSpec(memory_space=pl.ANY)
     dma = pltpu.SemaphoreType.DMA
     wide = 2 * STRIDE + HALO
     flows = pl.pallas_call(
         make_kernel(sizes, rows_each),
         out_shape=jax.ShapeDtypeStruct((rows_each, width), jnp.float32),
-        in_specs=[smem, smem] + [hbm] * 6,
+        in_specs=[hbm] * 8,
         out_specs=pl.BlockSpec(memory_space=pltpu.VMEM),
         scratch_shapes=[
             pltpu.VMEM((3, wide, wide), jnp.bfloat16),
@@ -398,8 +484,9 @@
             pltpu.VMEM((4, 2 * KROWS, wide), jnp.float32),
             pltpu.VMEM((2, 1, LAGS), jnp.float32),
             pltpu.VMEM((2 * count, 1, LAGS), jnp.float32),
-            dma((6,)), dma((8,)), dma((8,)), dma((8,)), dma((8,)), dma((5,)), dma((5,)),
-            dma(()), dma(()),
+            dma((9,)), dma((28,)), dma((28,)), dma((9,)), dma((9,)), dma(()), dma(()),
+            pltpu.SemaphoreType.REGULAR((len(doubling(sizes)) + 2,)),
+            pltpu.SMEM(priors.shape, priors.dtype), pltpu.SMEM(row_order.shape, row_order.dtype),
         ],
         compiler_params=pltpu.CompilerParams(
             vmem_limit_bytes=67043328, collective_id=0, has_side_effects=True

time: 35.1 us -> 31.7 us (0.903)
  Pallas kernels: 33.7 us -> 30.3 us
    pallas_call x1, Pallas kernels: 33.7 us -> 30.3 us  [body(): pl.pallas_call(make_kernel(sizes, rows_each), out_shape=jax.ShapeDtypeStr...]
where the time goes in v1:
time: 31.7 us; the launch traced here: 31.6 us
  Pallas kernels  30.3 us (96%)
  local copies, waits for them, and re-layouts  1.24 us (4%)
    pallas_call x1, Pallas kernels, body(): pl.pallas_call(make_kernel(sizes, rows_each), out_shape=jax.ShapeDtypeStr...  30.3 us
    unnamed x1, local copies, waits for them, and re-layouts  1.24 us

profile of v1, /device:TPU:0, one launch (start us, length us, event | category | flops | bytes accessed | tf_op | source)
XLA Modules:
  0.0 31.6 jit_solution(15528062499427783415)
XLA Ops:
  0.0 30.3 %shard_map.82 = f32[2,64]{1,0:T(2,128)} custom-call(s32[2,2,2,2]{3,2,1,0:T(2,128)} %pri_hbm.1, s32[8]{0:T(128)} %order_hbm.1, bf16[2,512,512]{2,1,0:T(8,128)(2,1)} %sec_hbm.1, bf16[544,512]{1,0:T(8,128)(2,1)} %constant.10.clone.dft_hbm, bf16[4,256,256]{2,1,0:T(8,128)(2,1)} %constant.11.clone.wg_hbm, f32[4,256,128]{2,1,0:T(8,128)} %constant.12.clone.colc_hbm, ...), custom_call_target="tpu_custom_call" | custom-call | tf_op jit(solution)/shard_map/pallas_call | solution.py:475
  30.3 1.2 %copy.10 = f32[2,64]{1,0:T(2,128)} copy(f32[2,64]{1,0:T(2,128)} %shard_map.82) | data formatting | bytes 1024

commit v2 on v1

--- a/solution.py
+++ b/solution.py
@@ -11,6 +11,7 @@
 PATCH = 512
 STRIDE = 256
 LAGS = 128
+MAXOFF = 64
 HALO = 256
 HALF = PATCH // 2
 QUARTER = PATCH // 4
@@ -41,16 +42,25 @@
     return np.stack(blocks)
 
 
-def lag_tables():
+def lag_table():
     lag = np.arange(2 * LAGS)[:, None] - LAGS
-    l = np.concatenate([4 * np.arange(QUARTER) + g for g in range(4)])[None, :]
     k = np.arange(KROWS)[None, :]
     weight = np.where(k == 0, 1.0, np.where(k < HALF, 2.0, np.where(k == HALF, 1.0, 0.0)))
-    col = (np.cos(angle_of(lag * l)), np.sin(angle_of(lag * l)))
     row_cos = np.cos(angle_of(lag * k)) * weight
     row_sin = -np.sin(angle_of(lag * k)) * weight
-    row = np.concatenate([row_cos, row_sin], axis=1)
-    return col[0], col[1], row
+    return np.concatenate([row_cos, row_sin], axis=1)
+
+
+def column_tables():
+    lag = np.arange(LAGS)[None, :] - LAGS // 2
+    shift = np.arange(-MAXOFF, MAXOFF + 1)[:, None]
+    matrix, phase = [], []
+    for g in range(4):
+        l = 4 * np.arange(QUARTER) + g
+        c, s = np.cos(angle_of(l[:, None] * lag)), np.sin(angle_of(l[:, None] * lag))
+        matrix.append(np.block([[c, s], [-s, c]]))
+        phase += [np.cos(angle_of(shift * l)), np.sin(angle_of(shift * l))]
+    return np.concatenate(matrix), np.concatenate(phase, axis=1)
 
 
 def bf16_const(value):
@@ -61,36 +71,45 @@
     return bf16_const(value).astype(np.float32)
 
 
-def first_pass(ext, section, i, dft_ref, pq_ref, slot, outer):
-    rows = pl.ds(pl.multiple_of(i * STRIDE, STRIDE), PATCH)
-    edge, far = HALO // 2, ext.shape[2] - HALO // 2
-    if not outer:
-        pq_ref[slot, :, edge:far] = jnp.dot(
-            dft_ref[...], ext[section, rows, edge:far], preferred_element_type=jnp.float32
-        )
-        return
-    window = jnp.concatenate([ext[section, rows, :edge], ext[section, rows, far:]], axis=1)
-    both = jnp.dot(dft_ref[...], window, preferred_element_type=jnp.float32)
-    pq_ref[slot, :, :edge] = both[:, :edge]
-    pq_ref[slot, :, far:] = both[:, edge:]
-
-
-def spectrum_pair(wg_ref, spec_ref, pq_ref, slot, base):
-    for j in range(2):
-        p, q = [], []
-        for t in range(4):
-            lanes = slice(j * STRIDE + t * QUARTER, j * STRIDE + (t + 1) * QUARTER)
-            p.append(pq_ref[slot, :KROWS, lanes])
-            q.append(pq_ref[slot, KROWS:, lanes])
-        ps, pd, qs, qd = p[0] + p[2], p[0] - p[2], q[0] + q[2], q[0] - q[2]
-        pt, pu, qt, qu = p[1] + p[3], p[1] - p[3], q[1] + q[3], q[1] - q[3]
-        groups = ((ps + pt, qs + qt), (pd + qu, qd - pu), (ps - pt, qs - qt), (pd - qu, qd + pu))
-        for g, (real, imag) in enumerate(groups):
-            left = jnp.concatenate([real.astype(jnp.bfloat16), imag.astype(jnp.bfloat16)], axis=1)
-            out = jnp.dot(left, wg_ref[g], preferred_element_type=jnp.float32).astype(jnp.bfloat16)
-            lo = g * QUARTER
-            spec_ref[base + j, :, lo : lo + QUARTER] = out[:, :QUARTER]
-            spec_ref[base + j, :, PATCH + lo : PATCH + lo + QUARTER] = out[:, QUARTER:]
+def first_pass(ext, section, dft_ref, pq_ref, slot, spans):
+    boxes = [(i, low, high) for i in range(2) for low, high in spans]
+    window = [ext[section, i * STRIDE : i * STRIDE + PATCH, low:high] for i, low, high in boxes]
+    both = jnp.dot(
+        dft_ref[...], jnp.concatenate(window, axis=1), preferred_element_type=jnp.float32
+    )
+    at = 0
+    for i, low, high in boxes:
+        pq_ref[slot + i, :, low:high] = both[:, at : at + high - low]
+        at += high - low
+
+
+def spectrum(wg_ref, pq_ref, slot, j):
+    p, q = [], []
+    for t in range(4):
+        lanes = slice(j * STRIDE + t * QUARTER, j * STRIDE + (t + 1) * QUARTER)
+        p.append(pq_ref[slot, :KROWS, lanes])
+        q.append(pq_ref[slot, KROWS:, lanes])
+    ps, pd, qs, qd = p[0] + p[2], p[0] - p[2], q[0] + q[2], q[0] - q[2]
+    pt, pu, qt, qu = p[1] + p[3], p[1] - p[3], q[1] + q[3], q[1] - q[3]
+    groups = ((ps + pt, qs + qt), (pd + qu, qd - pu), (ps - pt, qs - qt), (pd - qu, qd + pu))
+    for g, (real, imag) in enumerate(groups):
+        left = jnp.concatenate([real.astype(jnp.bfloat16), imag.astype(jnp.bfloat16)], axis=1)
+        out = jnp.dot(left, wg_ref[g], preferred_element_type=jnp.float32)
+        yield g, out[:, :QUARTER], out[:, QUARTER:]
+
+
+def spectrum_work(wg_ref, pq_ref, slot, j, turn_ref, at, cross_ref, phase):
+    for g, re, im in spectrum(wg_ref, pq_ref, slot, j):
+        low, mid, high = 2 * g * QUARTER, (2 * g + 1) * QUARTER, (2 * g + 2) * QUARTER
+        if cross_ref is not None:
+            ar, ai = turn_ref[at, :, low:mid], turn_ref[at, :, mid:high]
+            cross_ref[at, :, low:mid] = (ar * re + ai * im).astype(jnp.bfloat16)
+            cross_ref[at, :, mid:high] = (ar * im - ai * re).astype(jnp.bfloat16)
+        if phase is not None:
+            c, s = phase[:, low:mid], phase[:, mid:high]
+            turn_ref[at, :, low:mid] = re * c + im * s
+            turn_ref[at, :, mid:high] = im * c - re * s
+        yield
 
 
 def lag_rows(table, prior):
@@ -107,26 +126,24 @@
     return np.stack(np.split(table, width // LAGS, axis=1))
 
 
-def pair_flow(first, second, p, q, spec_ref, colc_ref, cols_ref, row_ref):
+def half_work(cross_ref, n, e_ref, halves):
+    total = None
+    for g in range(4):
+        part = slice(2 * g * QUARTER, 2 * (g + 1) * QUARTER)
+        piece = jnp.dot(cross_ref[n, :, part], e_ref[part], preferred_element_type=jnp.float32)
+        total = piece if total is None else total + piece
+        if g == 3:
+            halves[n] = total.astype(jnp.bfloat16)
+        yield
+
+
+def surface_of(half, rows):
+    stacked = jnp.concatenate([half[:, :LAGS], half[:, LAGS:]], axis=0)
+    return jnp.dot(rows, stacked, preferred_element_type=jnp.float32) * (1.0 / PATCH**3)
+
+
+def centroid(surface, p, q):
     f32 = jnp.float32
-    ar = spec_ref[first, :, :PATCH].astype(f32)
-    ai = spec_ref[first, :, PATCH:].astype(f32)
-    br = spec_ref[second, :, :PATCH].astype(f32)
-    bi = spec_ref[second, :, PATCH:].astype(f32)
-    cr = (ar * br + ai * bi).astype(jnp.bfloat16)
-    ci = (ar * bi - ai * br).astype(jnp.bfloat16)
-    ec = lag_rows(colc_ref, q)
-    es = lag_rows(cols_ref, q)
-    left = jnp.concatenate([cr, ci], axis=1)
-    right = jnp.concatenate(
-        [jnp.concatenate([ec, -es], axis=1), jnp.concatenate([es, ec], axis=1)], axis=0
-    )
-    half = lax.dot_general(
-        left, right, (((1,), (1,)), ((), ())), preferred_element_type=f32
-    ).astype(jnp.bfloat16)
-    stacked = jnp.concatenate([half[:, :LAGS], half[:, LAGS:]], axis=0)
-    rows = lag_rows(row_ref, p)[:, : 2 * KROWS]
-    surface = jnp.dot(rows, stacked, preferred_element_type=f32) * (1.0 / PATCH**3)
     w = surface * surface
     da = (lax.broadcasted_iota(jnp.int32, (LAGS, LAGS), 0) - LAGS // 2).astype(f32)
     db = (lax.broadcasted_iota(jnp.int32, (1, LAGS), 1) - LAGS // 2).astype(f32)
@@ -135,6 +152,11 @@
     row_m = jnp.sum(jnp.sum(w * da, axis=0, keepdims=True), axis=1, keepdims=True)
     col_m = jnp.sum(col_w * db, axis=1, keepdims=True)
     return p.astype(f32) + row_m / total, q.astype(f32) + col_m / total
+
+
+def interleave(*works):
+    for _ in zip(*works):
+        pass
 
 
 def make_kernel(sizes, rows_each):
@@ -165,8 +187,9 @@
         return [n for n, c in enumerate(copies) if c[0] == section and c[1] in kinds]
 
     def kernel(
-        pri_hbm, order_hbm, sec_hbm, dft_hbm, wg_hbm, colc_hbm, cols_hbm, row_hbm, out_ref,
-        ext, dft_ref, wg_ref, colc_ref, cols_ref, row_ref, spec_ref, pq_ref, mine_ref, all_ref,
+        pri_hbm, order_hbm, sec_hbm, dft_hbm, wg_hbm, e_hbm, phase_hbm, row_hbm, out_ref,
+        ext, dft_ref, wg_ref, e_ref, phase_ref, row_ref, turn_ref, cross_ref, lags_ref, pq_ref,
+        mine_ref, all_ref,
         load_sem, halo_send, halo_recv, chunk_send, chunk_recv, flow_send, flow_recv, flood, pri_ref,
         order_ref,
     ):
@@ -218,8 +241,8 @@
             for n in range(2)
         ]
         tables = (
-            (dft_hbm, dft_ref), (wg_hbm, wg_ref), (colc_hbm, colc_ref), (cols_hbm, cols_ref),
-            (row_hbm, row_ref), (pri_hbm, pri_ref), (order_hbm, order_ref),
+            (dft_hbm, dft_ref), (wg_hbm, wg_ref), (row_hbm, row_ref), (pri_hbm, pri_ref),
+            (order_hbm, order_ref), (e_hbm, e_ref), (phase_hbm, phase_ref),
         )
         for n, (source, target) in enumerate(tables):
             loads.append(pltpu.make_async_copy(source, target, load_sem.at[n + 2]))
@@ -310,13 +333,69 @@
                     climb(n + 1)
             done[0] = max(done[0], min(upto, rounds))
 
-        def middle(n, carry):
-            first_pass(ext, n // 2, n % 2, dft_ref, pq_ref, n % 4, False)
-            return carry
-
-        def spectra(n, carry):
-            first_pass(ext, n // 2, n % 2, dft_ref, pq_ref, n % 4, True)
-            spectrum_pair(wg_ref, spec_ref, pq_ref, n % 4, n * 2)
+        wide = ext.shape[2]
+        edge, last = margin, wide - margin
+        spans_of = {
+            "middle": ((edge, last),),
+            "outer": ((0, edge), (last, wide)),
+            "sides": ((0, 2 * edge), (last - edge, wide)),
+            "center": ((2 * edge, last - edge),),
+        }
+
+        def columns_pass(section, part):
+            first_pass(ext, section, dft_ref, pq_ref, 2 * (section % 2), spans_of[part])
+
+        lane = lax.broadcasted_iota(jnp.int32, (1, LAGS), 1)
+        sections, columns = 2 * size_gz, 2 * size_col
+
+        def prior(part, section, i, j):
+            return pri_ref[part, section, i, j]
+
+        def patch(section, i, j):
+            phase = None
+            if section < 2:
+                phase = phase_ref[pl.ds(prior(1, section, i, j) + MAXOFF, 1), :]
+            return spectrum_work(
+                wg_ref, pq_ref, 2 * (section % 2) + i, j, turn_ref, 2 * i + j,
+                cross_ref if section else None, phase,
+            )
+
+        def flows(section, surfaces):
+            values = []
+            for n in range(4):
+                p, q = prior(0, section - 1, n // 2, n % 2), prior(1, section - 1, n // 2, n % 2)
+                a, b = centroid(surfaces[n], p, q)
+                at = (2 * gz + section - 1) * columns + 2 * col + n % 2
+                value = jnp.where(lane == at, a, 0.0)
+                values.append(value + jnp.where(lane == at + sections * columns, b, 0.0))
+            mine_ref[0] = mine_ref[0] + values[0] + values[1]
+            mine_ref[1] = mine_ref[1] + values[2] + values[3]
+
+        def patches(section):
+            halves, surfaces = {}, {}
+
+            def spectra(i):
+                return [patch(section, i, j) for j in range(2)]
+
+            def half(i):
+                return [half_work(cross_ref, 2 * i + j, e_ref, halves) for j in range(2)]
+
+            def surface(i):
+                for n in (2 * i, 2 * i + 1):
+                    surfaces[n] = surface_of(halves[n], lags_ref[4 * (section - 1) + n])
+
+            interleave(*spectra(0))
+            if not section:
+                interleave(*spectra(1))
+                return
+            interleave(*half(0), *spectra(1))
+            interleave(*half(1))
+            surface(0)
+            surface(1)
+            flows(section, surfaces)
+
+        def lag_prepare(n, carry):
+            lags_ref[n] = lag_rows(row_ref, prior(0, n // 4, (n // 2) % 2, n % 2))[:, : 2 * KROWS]
             return carry
 
         for step in cross + diagonal:
@@ -339,35 +418,16 @@
         for copy in loads[2:]:
             copy.wait()
 
-        lane = lax.broadcasted_iota(jnp.int32, (1, LAGS), 1)
-        sections, columns = 2 * size_gz, 2 * size_col
-
-        def prior(part, n):
-            return pri_ref[part, n // 4, (n // 2) % 2, n % 2]
-
-        def pairs_static(low, high):
-            values = []
-            for n in range(low, high):
-                a, b = pair_flow(
-                    n, n + 4, prior(0, n), prior(1, n), spec_ref, colc_ref, cols_ref, row_ref
-                )
-                at = (2 * gz + n // 4) * columns + 2 * col + n % 2
-                values.append(
-                    jnp.where(lane == at, a, 0.0)
-                    + jnp.where(lane == at + sections * columns, b, 0.0)
-                )
-            mine_ref[0] = mine_ref[0] + values[0] + values[1]
-            mine_ref[1] = mine_ref[1] + values[2] + values[3]
-
+        lax.fori_loop(0, 8, lag_prepare, 0)
         arrive(pick(0, "row"))
-        lax.fori_loop(0, 2, middle, 0, unroll=2)
+        columns_pass(0, "middle")
         spread(1)
         took(0, 4)
         send(pick(2, "diagonal", "corner"))
         arrive(pick(0, "col"))
         send(pick(0, "turn"))
         arrive(pick(1, "row"))
-        lax.fori_loop(2, 4, middle, 0, unroll=2)
+        columns_pass(1, "middle")
         spread(2)
         took(4, 5)
         send(pick(2, "left"))
@@ -376,21 +436,22 @@
         took(5, 6)
         send(pick(2, "right"))
         arrive(pick(0, "turn"))
-        lax.fori_loop(0, 2, spectra, 0, unroll=2)
+        columns_pass(0, "outer")
+        patches(0)
         spread(3)
         took(6, 7)
         send(pick(2, "up"))
         took(7, 8)
         send(pick(2, "down"))
         arrive(pick(1, "turn"))
-        lax.fori_loop(2, 4, spectra, 0, unroll=2)
-        pairs_static(0, 4)
+        columns_pass(1, "outer")
+        patches(1)
+        arrive(pick(2, "left", "right", "diagonal", "corner"))
+        columns_pass(2, "sides")
         took(8, 9)
-        arrive(pick(2, "up", "down", "corner"))
-        lax.fori_loop(4, 6, middle, 0, unroll=2)
-        arrive(pick(2, "left", "right", "diagonal"))
-        lax.fori_loop(4, 6, spectra, 0, unroll=2)
-        pairs_static(4, 8)
+        arrive(pick(2, "up", "down"))
+        columns_pass(2, "center")
+        patches(2)
         spread(rounds)
 
         total_rows = 2 * size_row
@@ -461,13 +522,13 @@
     count = math.prod(sizes)
     rows_each = row_order.shape[0] // sizes[1]
     width = 2 * 2 * sizes[0] * 2 * sizes[2]
-    colc, cols, row = lag_tables()
+    matrix, phase = column_tables()
     tables = (
         bf16_const(dft_table()),
         bf16_const(split_tables()),
-        f32_const(lane_tiles(colc)),
-        f32_const(lane_tiles(cols)),
-        f32_const(lane_tiles(row)),
+        bf16_const(matrix),
+        phase.astype(np.float32),
+        f32_const(lane_tiles(lag_table())),
     )
     hbm = pl.BlockSpec(memory_space=pl.ANY)
     dma = pltpu.SemaphoreType.DMA
@@ -480,7 +541,9 @@
         scratch_shapes=[
             pltpu.VMEM((3, wide, wide), jnp.bfloat16),
             *[pltpu.VMEM(t.shape, t.dtype) for t in tables],
-            pltpu.VMEM((12, KROWS, 2 * PATCH), jnp.bfloat16),
+            pltpu.VMEM((4, KROWS, 2 * PATCH), jnp.float32),
+            pltpu.VMEM((4, KROWS, 2 * PATCH), jnp.bfloat16),
+            pltpu.VMEM((8, LAGS, 2 * KROWS), jnp.bfloat16),
             pltpu.VMEM((4, 2 * KROWS, wide), jnp.float32),
             pltpu.VMEM((2, 1, LAGS), jnp.float32),
             pltpu.VMEM((2 * count, 1, LAGS), jnp.float32),
@@ -489,9 +552,9 @@
             pltpu.SMEM(priors.shape, priors.dtype), pltpu.SMEM(row_order.shape, row_order.dtype),
         ],
         compiler_params=pltpu.CompilerParams(
-            vmem_limit_bytes=67043328, collective_id=0, has_side_effects=True
+            vmem_limit_bytes=41943040, collective_id=0, has_side_effects=True
         ),
-    )(priors, row_order, sections, *tables)
+    )(*[pltpu.with_memory_space_constraint(x, pltpu.HBM) for x in (priors, row_order, sections, *tables)])
     return flows
 
 

time: 31.7 us -> 28.3 us (0.89)
  Pallas kernels: 30.3 us -> 27.6 us
  local copies, waits for them, and re-layouts: 1.24 us -> 0.56 us
    pallas_call x1, Pallas kernels: 30.3 us -> 27.6 us  [body(): pl.pallas_call(make_kernel(sizes, rows_each), out_shape=jax.ShapeDtypeStr...]
    unnamed x1, local copies, waits for them, and re-layouts: 1.24 us -> 0.56 us
where the time goes in v2:
time: 28.3 us; the launch traced here: 28.2 us
  Pallas kernels  27.6 us (98%)
  local copies, waits for them, and re-layouts  0.56 us (2%)
    pallas_call x1, Pallas kernels, body(): pl.pallas_call(make_kernel(sizes, rows_each), out_shape=jax.ShapeDtypeStr...  27.6 us

profile of v2, /device:TPU:0, one launch (start us, length us, event | category | flops | bytes accessed | tf_op | source)
XLA Modules:
  0.0 28.2 jit_solution(5751075636474144844)
XLA Ops:
  0.0 27.6 %shard_map.82 = f32[2,64]{1,0:T(2,128)S(1)} custom-call(s32[2,2,2,2]{3,2,1,0:T(2,128)} %pri_hbm.1, s32[8]{0:T(128)} %order_hbm.1, bf16[2,512,512]{2,1,0:T(8,128)(2,1)} %sec_hbm.1, bf16[544,512]{1,0:T(8,128)(2,1)} %constant.10.clone.dft_hbm, bf16[4,256,256]{2,1,0:T(8,128)(2,1)} %constant.11.clone.wg_hbm, bf16[1024,256]{1,0:T(8,128)(2,1)} %constant.12.clone.e_hbm, ...), custom_call_target="tpu_custom_call" | custom-call | tf_op jit(solution)/shard_map/pallas_call | solution.py:536
  27.6 0.6 %copy.10 = f32[2,64]{1,0:T(2,128)} copy(f32[2,64]{1,0:T(2,128)S(1)} %shard_map.82) | data formatting | bytes 1024

commit v3 on v2

--- a/solution.py
+++ b/solution.py
@@ -267,8 +267,13 @@
             )
 
         def guard(n, sign):
-            (a, b), side_col = copies[n][2], copies[n][3]
-            return exists((sign * a, side_col if side_col else sign * b))
+            _, kind, (a, b), side_col, _ = copies[n]
+            if kind == "swing":
+                return jnp.logical_and(row % 2 == 1, exists((1, sign * b)))
+            ok = exists((sign * a, side_col if side_col else sign * b))
+            if kind == "turn" and a < 0:
+                ok = jnp.logical_and(ok, row % 2 == (1 if sign > 0 else 0))
+            return ok
 
         def send(numbers):
             for n in numbers:
@@ -371,7 +376,7 @@
             mine_ref[0] = mine_ref[0] + values[0] + values[1]
             mine_ref[1] = mine_ref[1] + values[2] + values[3]
 
-        def patches(section):
+        def patches(section, event=None):
             halves, surfaces = {}, {}
 
             def spectra(i):
@@ -388,6 +393,8 @@
             if not section:
                 interleave(*spectra(1))
                 return
+            if event is not None:
+                event()
             interleave(*half(0), *spectra(1))
             interleave(*half(1))
             surface(0)
@@ -418,15 +425,25 @@
         for copy in loads[2:]:
             copy.wait()
 
+        def top():
+            took(6, 7)
+            send(pick(2, "up"))
+
+        def bottom():
+            took(7, 8)
+            send(pick(2, "down"))
+
         lax.fori_loop(0, 8, lag_prepare, 0)
         arrive(pick(0, "row"))
+        send(pick(0, "swing"))
         columns_pass(0, "middle")
         spread(1)
-        took(0, 4)
-        send(pick(2, "diagonal", "corner"))
         arrive(pick(0, "col"))
         send(pick(0, "turn"))
         arrive(pick(1, "row"))
+        send(pick(1, "swing"))
+        took(0, 4)
+        send(pick(2, "diagonal", "corner"))
         columns_pass(1, "middle")
         spread(2)
         took(4, 5)
@@ -435,17 +452,14 @@
         send(pick(1, "turn"))
         took(5, 6)
         send(pick(2, "right"))
-        arrive(pick(0, "turn"))
+        arrive(pick(0, "turn", "swing"))
         columns_pass(0, "outer")
         patches(0)
         spread(3)
-        took(6, 7)
-        send(pick(2, "up"))
-        took(7, 8)
-        send(pick(2, "down"))
-        arrive(pick(1, "turn"))
+        top()
+        arrive(pick(1, "turn", "swing"))
         columns_pass(1, "outer")
-        patches(1)
+        patches(1, bottom)
         arrive(pick(2, "left", "right", "diagonal", "corner"))
         columns_pass(2, "sides")
         took(8, 9)
@@ -506,6 +520,8 @@
             copies.append((section, kind, step, 0, span[step[0]] + span[step[1]]))
         for a, b in diagonal:
             copies.append((section, "turn", (a, 0), b, span[a] + halo[b]))
+        for b in (-1, 1):
+            copies.append((section, "swing", (0, b), 0, halo[1] + span[b]))
     for a, b in diagonal:
         copies.append((2, "diagonal", (a, b), 0, span[a] + span[b]))
     for a, b in diagonal:
@@ -547,7 +563,7 @@
             pltpu.VMEM((4, 2 * KROWS, wide), jnp.float32),
             pltpu.VMEM((2, 1, LAGS), jnp.float32),
             pltpu.VMEM((2 * count, 1, LAGS), jnp.float32),
-            dma((9,)), dma((28,)), dma((28,)), dma((9,)), dma((9,)), dma(()), dma(()),
+            dma((9,)), dma((32,)), dma((32,)), dma((9,)), dma((9,)), dma(()), dma(()),
             pltpu.SemaphoreType.REGULAR((len(doubling(sizes)) + 2,)),
             pltpu.SMEM(priors.shape, priors.dtype), pltpu.SMEM(row_order.shape, row_order.dtype),
         ],

time: 28.3 us -> 27.5 us (0.972)
  Pallas kernels: 27.6 us -> 26.8 us
    pallas_call x1, Pallas kernels: 27.6 us -> 26.8 us  [body(): pl.pallas_call(make_kernel(sizes, rows_each), out_shape=jax.ShapeDtypeStr...]
where the time goes in v3:
time: 27.5 us; the launch traced here: 27.4 us
  Pallas kernels  26.8 us (97%)
  local copies, waits for them, and re-layouts  0.56 us (2%)
    pallas_call x1, Pallas kernels, body(): pl.pallas_call(make_kernel(sizes, rows_each), out_shape=jax.ShapeDtypeStr...  26.8 us
    unnamed x1, local copies, waits for them, and re-layouts  0.56 us

profile of v3, /device:TPU:0, one launch (start us, length us, event | category | flops | bytes accessed | tf_op | source)
XLA Modules:
  0.0 27.4 jit_solution(3924591900372687266)
XLA Ops:
  0.0 26.8 %shard_map.82 = f32[2,64]{1,0:T(2,128)S(1)} custom-call(s32[2,2,2,2]{3,2,1,0:T(2,128)} %pri_hbm.1, s32[8]{0:T(128)} %order_hbm.1, bf16[2,512,512]{2,1,0:T(8,128)(2,1)} %sec_hbm.1, bf16[544,512]{1,0:T(8,128)(2,1)} %constant.10.clone.dft_hbm, bf16[4,256,256]{2,1,0:T(8,128)(2,1)} %constant.11.clone.wg_hbm, bf16[1024,256]{1,0:T(8,128)(2,1)} %constant.12.clone.e_hbm, ...), custom_call_target="tpu_custom_call" | custom-call | tf_op jit(solution)/shard_map/pallas_call | solution.py:552
  26.8 0.6 %copy.10 = f32[2,64]{1,0:T(2,128)} copy(f32[2,64]{1,0:T(2,128)S(1)} %shard_map.82) | data formatting | bytes 1024
